TPU v7x, 32 devices: a whole 2x2x4 slice. The times are simulated.
32 devices in a mesh: lat: 8 (over z, y), lon: 4 (over x, core).
Axes of the slice: x: 2, y: 2, z: 4, core: 2. Of those that a mesh axis runs over, the one named last changes fastest.
Arguments:
- field: bfloat16 [150, 128, 1024], P(None, 'lat', 'lon'), may hold values from -6 to 6
- land_mask: int32 [128, 1024], P('lat', 'lon'), may hold values 0 or 1
- fold_partner: int32 [1024], replicated, may hold values from 0 to 1023, as said below
- dw_kernel: float32 [150, 7, 7], replicated, may hold values from -0.875 to 0.875
- norm_gain: float32 [150], replicated, may hold values from 0.1 to 1.9
- w_in: bfloat16 [150, 600], replicated, may hold values from -0.5 to 0.5
- w_out: bfloat16 [600, 150], replicated, may hold values from -0.25 to 0.25
- spec_gain: float32 [2, 150, 512], replicated, may hold values from -12 to 12
- mix_weight: bfloat16 [150, 150], replicated, may hold values from -0.5 to 0.5
Outputs:
- block_out: bfloat16 [150, 128, 1024], P(None, 'lat', 'lon')
Inputs may be any that keep to these rules, and one draw needn't show every extreme that they name: There is one s such that fold_partner[j] = (s - j) mod 1024 for every j.
All inputs are finite; a program needn't handle non-finite values. No bound on the sum of `land_mask` on one device may be relied on, other than what follows from the above.
Results may differ from a plain program's by a relative error of at most 0.0065.
Values may be sent and summed in bfloat16 or wider, within the bound.
A program may use at most 128 MiB of HBM per device.

v0:
```python
import functools
import math

import jax
import jax.numpy as jnp
import numpy as np
from jax import lax
from jax.experimental import pallas as pl
from jax.experimental.pallas import tpu as pltpu
from jax.sharding import PartitionSpec as P

F32 = jnp.float32
BF16 = jnp.bfloat16
TAPS = 7
HALO = 3
LANES = 128


def dft_table(lon_points, mode_count):
    phase = np.arange(lon_points)[:, None] * np.arange(mode_count)[None, :] % lon_points
    angles = phase.astype(np.float32) * np.float32(2.0 * math.pi / lon_points)
    factor = np.float32(1.0 / math.sqrt(lon_points))
    angles = angles.astype(np.float64)
    table = np.concatenate([np.cos(angles), -np.sin(angles)], axis=1).astype(np.float32)
    return (table * factor).astype(BF16)


def kernel(
    sizes,
    field_ref, mask_ref, fold_ref, taps_ref, gain_ref, w_in_ref, w_out_ref, mix_ref, spec_hbm, table_hbm,
    out_ref,
    flat, ext, own, depth, res, by_rows, back, spatial,
    edge_mine, edge_left, edge_right, comb, comb_n, comb_s, rows_n, rows_s, top_all,
    spec_ref, table_ref, wide_taps, w_in_t, w_out_t, mix_t, gain_col,
    local_sem, edge_send, edge_recv, comb_send, comb_recv, rows_send, rows_recv,
    fold_send, fold_recv, out_send, out_recv, in_send, in_recv,
):
    channels, padded, rows, cols, lat_n, lon_n, modes = sizes
    lon_points = cols * lon_n
    per = rows // lon_n
    lat = lax.axis_index("lat")
    lon = lax.axis_index("lon")
    left = lax.rem(lon + lon_n - 1, lon_n)
    right = lax.rem(lon + 1, lon_n)
    chip = lon // 2
    core = lax.rem(lon, 2)
    chips = lon_n // 2

    def target(k):
        return lax.rem(chip + k // 2, chips) * 2 + lax.rem(core + lax.rem(k, 2), 2)

    def source(k):
        return lax.rem(chip + chips - k // 2, chips) * 2 + lax.rem(core + lax.rem(k, 2), 2)

    table_copy = pltpu.make_async_copy(table_hbm, table_ref, local_sem.at[0])
    spec_copy = pltpu.make_async_copy(spec_hbm, spec_ref, local_sem.at[1])
    table_copy.start()
    spec_copy.start()

    barrier = pltpu.get_barrier_semaphore()
    for k in range(1, lon_n):
        pl.semaphore_signal(barrier, inc=1, device_id={"lon": target(k)})

    @pl.when(lat > 0)
    def _():
        pl.semaphore_signal(barrier, inc=1, device_id={"lat": lat - 1})

    @pl.when(lat < lat_n - 1)
    def _():
        pl.semaphore_signal(barrier, inc=1, device_id={"lat": lat + 1})

    wet = mask_ref[...].astype(F32)

    @pl.loop(0, channels)
    def _(c):
        val = field_ref[c].astype(F32) * wet
        at = pl.multiple_of(c * rows, rows)
        flat[0, pl.ds(at, rows), :] = val[:, :LANES]
        flat[1, pl.ds(at, rows), :] = val[:, LANES:]

    tail = (padded - channels) * rows
    if tail:
        for h in range(2):
            flat[h, channels * rows :, :] = jnp.zeros((tail, LANES), F32)

    lane = lax.broadcasted_iota(jnp.int32, (padded, LANES), 1)
    pack = jnp.zeros((padded, LANES), F32)
    edge_mine[...] = pack.astype(BF16)
    for i in range(rows):
        lo = flat[0, pl.ds(i, padded, stride=rows), :]
        hi = flat[1, pl.ds(i, padded, stride=rows), :]
        own[i, :, :LANES] = lo.astype(BF16)
        own[i, :, LANES:] = hi.astype(BF16)
        ext[i + HALO, :, :LANES] = lo
        ext[i + HALO, :, LANES : 2 * LANES] = hi
        edge = jnp.where(lane < HALO, lo, jnp.where(lane >= LANES - HALO, hi, 0.0))
        if i:
            edge = pltpu.roll(edge, 8 * i, 1)
        edge_mine[...] = (edge_mine[...].astype(F32) + edge).astype(BF16)

    count = lon_n - 1 + jnp.where(lat > 0, 1, 0) + jnp.where(lat < lat_n - 1, 1, 0)
    pl.semaphore_wait(barrier, count)

    to_left = pltpu.make_async_remote_copy(
        edge_mine, edge_right, edge_send.at[0], edge_recv.at[0], device_id={"lon": left})
    to_right = pltpu.make_async_remote_copy(
        edge_mine, edge_left, edge_send.at[1], edge_recv.at[1], device_id={"lon": right})
    to_left.start()
    to_right.start()

    rows_down = pltpu.make_async_remote_copy(
        own.at[pl.ds(0, HALO)], rows_n, rows_send.at[0], rows_recv.at[0], device_id={"lat": lat - 1})
    rows_up = pltpu.make_async_remote_copy(
        own.at[pl.ds(rows - HALO, HALO)], rows_s, rows_send.at[1], rows_recv.at[1], device_id={"lat": lat + 1})
    comb_down = pltpu.make_async_remote_copy(
        comb, comb_n, comb_send.at[0], comb_recv.at[0], device_id={"lat": lat - 1})
    comb_up = pltpu.make_async_remote_copy(
        comb, comb_s, comb_send.at[1], comb_recv.at[1], device_id={"lat": lat + 1})

    def fold_copy(k):
        at = pl.multiple_of(lon * cols, LANES)
        return pltpu.make_async_remote_copy(
            own.at[pl.ds(rows - HALO, HALO)], top_all.at[:, :, pl.ds(at, cols)],
            fold_send.at[k - 1], fold_recv.at[k - 1], device_id={"lon": target(k)})

    @pl.when(lat > 0)
    def _():
        rows_down.start()

    @pl.when(lat < lat_n - 1)
    def _():
        rows_up.start()

    @pl.when(lat == lat_n - 1)
    def _():
        for k in range(lon_n - 1, 0, -1):
            fold_copy(k).start()
        top_all[:, :, pl.ds(pl.multiple_of(lon * cols, LANES), cols)] = own[rows - HALO :]

    wide_taps[:, padded - 16 :, :] = jnp.zeros((TAPS * TAPS, 16, LANES), F32)
    chan_up = -(-channels // LANES) * LANES
    for a in range(TAPS):
        line = jnp.concatenate([taps_ref[a], jnp.zeros((TAPS, chan_up - channels), F32)], axis=1)
        line = jnp.concatenate([line, jnp.zeros((LANES - TAPS, chan_up), F32)], axis=0).T
        for b in range(TAPS):
            wide_taps[a * TAPS + b, :channels, :] = jnp.broadcast_to(line[:channels, b : b + 1], (channels, LANES))

    def turned(ref, target_ref):
        n, m = ref.shape
        up = [-(-d // LANES) * LANES for d in (n, m)]
        full = jnp.concatenate([ref[...].astype(F32), jnp.zeros((n, up[1] - m), F32)], axis=1)
        full = jnp.concatenate([full, jnp.zeros((up[0] - n, up[1]), F32)], axis=0)
        target_ref[...] = full.T[: target_ref.shape[0], : target_ref.shape[1]].astype(BF16)

    turned(w_in_ref, w_in_t)
    hid = w_out_ref.shape[1]
    w_out_t[...] = jnp.zeros(w_out_t.shape, BF16)
    w_out_t[:channels, :hid] = w_out_ref[...]
    turned(mix_ref, mix_t)
    diagonal = lax.broadcasted_iota(jnp.int32, (padded, channels), 0) == lax.broadcasted_iota(
        jnp.int32, (padded, channels), 1)
    gain_col[...] = jnp.broadcast_to(
        jnp.sum(jnp.where(diagonal, gain_ref[...], 0.0), axis=1, keepdims=True), (padded, LANES))
    back[:, padded - 16 :, :] = jnp.zeros((per, 16, lon_points), BF16)

    to_left.wait()
    to_right.wait()
    both = jnp.where(lax.rem(lane, 8) < 4, edge_right[...].astype(F32), edge_left[...].astype(F32))
    comb[...] = both.astype(BF16)

    @pl.when(lat > 0)
    def _():
        comb_down.start()

    @pl.when(lat < lat_n - 1)
    def _():
        comb_up.start()

    def edges_of(packed, i):
        return pltpu.roll(packed, LANES - 8 * i, 1) if i else packed

    for i in range(rows):
        ext[i + HALO, :, 2 * LANES :] = edges_of(comb[...].astype(F32), i)

    def conv(out_rows):
        lines = sorted({i + a for i in out_rows for a in range(TAPS)})

        @pl.loop(0, padded // 16)
        def _(group):
            for half in range(2):
                at = pl.multiple_of(group * 16 + half * 8, 8)
                acc = {}
                for b in range(TAPS):
                    weights = [wide_taps[a * TAPS + b, pl.ds(at, 8), :] for a in range(TAPS)]
                    for e in lines:
                        line = ext[e, pl.ds(at, 8), :]
                        if b != HALO:
                            line = pltpu.roll(line, (HALO - b) % (cols + LANES), 1)
                        for a in range(TAPS):
                            i = e - a
                            if i in out_rows:
                                for h in range(cols // LANES):
                                    term = weights[a] * line[:, h * LANES : (h + 1) * LANES]
                                    acc[i, h] = acc[i, h] + term if (i, h) in acc else term
                for (i, h), total in acc.items():
                    depth[i, pl.ds(at, 8), h * LANES : (h + 1) * LANES] = total

    def await_halo():
        @pl.when(lat > 0)
        def _():
            rows_down.wait_send()
            comb_down.wait_send()
            rows_up.wait_recv()
            comb_up.wait_recv()
            for r in range(HALO):
                ext[r, :, :cols] = rows_s[r].astype(F32)
                ext[r, :, cols:] = edges_of(comb_s[...].astype(F32), rows - HALO + r)

        @pl.when(lat == 0)
        def _():
            for r in range(HALO):
                ext[r] = jnp.zeros((padded, cols + LANES), F32)

        @pl.when(lat < lat_n - 1)
        def _():
            rows_up.wait_send()
            comb_up.wait_send()
            rows_down.wait_recv()
            comb_down.wait_recv()
            for r in range(HALO):
                ext[rows + HALO + r, :, :cols] = rows_n[r].astype(F32)
                ext[rows + HALO + r, :, cols:] = edges_of(comb_n[...].astype(F32), r)

        @pl.when(lat == lat_n - 1)
        def _():
            for k in range(lon_n - 1, 0, -1):
                fold_copy(k).wait()
            point = lax.broadcasted_iota(jnp.int32, (lon_points, cols + LANES), 0)
            at = lax.broadcasted_iota(jnp.int32, (1, cols + LANES), 1)
            at = jnp.where(at < cols + HALO, at, at - (cols + LANES)) + lon * cols
            mate = fold_ref[:, :1] - at
            mate = jnp.where(mate < 0, mate + lon_points, mate)
            mate = jnp.where(mate < 0, mate + lon_points, mate)
            mate = jnp.where(mate >= lon_points, mate - lon_points, mate)
            pick = jnp.where(point == mate, 1.0, 0.0).astype(BF16)
            for r in range(HALO):
                ext[rows + HALO + r] = jnp.dot(top_all[HALO - 1 - r], pick, preferred_element_type=F32)

    here = pl.ds(pl.multiple_of(lon * cols, LANES), cols)

    def row_at(chunk, q):
        return lax.rem(chunk * lon_n + q + HALO, rows)

    def send_row(chunk, k):
        s = chunk * (lon_n - 1) + lon_n - 1 - k
        return pltpu.make_async_remote_copy(
            res.at[row_at(chunk, target(k))], by_rows.at[chunk, :, here],
            out_send.at[s], out_recv.at[s], device_id={"lon": target(k)})

    def send_back(chunk, k):
        q = target(k)
        s = chunk * (lon_n - 1) + lon_n - 1 - k
        return pltpu.make_async_remote_copy(
            back.at[chunk, :, pl.ds(pl.multiple_of(q * cols, LANES), cols)], spatial.at[chunk * lon_n + lon],
            in_send.at[s], in_recv.at[s], device_id={"lon": q})

    inside = lax.broadcasted_iota(jnp.int32, (padded, 2 * cols), 0) < channels

    def mix_rows(chunk):
        @pl.loop(0, lon_n // 2)
        def _(pair):
            k = lon_n - 1 - 2 * pair
            one, two = row_at(chunk, target(k)), row_at(chunk, target(k - 1))
            x = jnp.concatenate([depth[one], depth[two]], axis=1)
            mean = jnp.sum(x, axis=0, keepdims=True) * (1.0 / channels)
            centred = jnp.where(inside, x - mean, 0.0)
            var = jnp.sum(centred * centred, axis=0, keepdims=True) * (1.0 / channels)
            normed = (centred * lax.rsqrt(var + 1e-06) * gain_col[:, :1]).astype(BF16)
            pre = jnp.dot(w_in_t[...], normed, preferred_element_type=F32)
            hidden = jax.nn.gelu(pre, approximate=True).astype(BF16)
            branch = jnp.dot(w_out_t[...], hidden, preferred_element_type=F32)
            for n, row in enumerate((one, two)):
                wet_row = mask_ref[pl.ds(row, 1), :].astype(F32)
                part = branch[:, n * cols : (n + 1) * cols]
                res[row] = (wet_row * (own[row].astype(F32) + part)).astype(BF16)
            send_row(chunk, k).start()

            @pl.when(pair < lon_n // 2 - 1)
            def _():
                send_row(chunk, k - 1).start()

            @pl.when(pair == lon_n // 2 - 1)
            def _():
                by_rows[chunk, :, here] = res[two]

    def spectral(chunk):
        for k in range(lon_n - 1, 0, -1):
            send_row(chunk, k).wait_recv()
        spectrum = jnp.dot(by_rows[chunk], table_ref[...], preferred_element_type=F32)
        s_re = spectrum[:channels, :modes]
        s_im = spectrum[:channels, modes:]
        g_re = spec_ref[0]
        g_im = spec_ref[1]
        scaled = jnp.concatenate(
            [(g_re * s_re - g_im * s_im).astype(BF16), (g_re * s_im + g_im * s_re).astype(BF16)], axis=1)
        back[chunk, :channels] = lax.dot_general(
            scaled, table_ref[...], (((1,), (1,)), ((), ())), preferred_element_type=F32).astype(BF16)
        for k in range(lon_n - 1, 0, -1):
            send_back(chunk, k).start()
        spatial[chunk * lon_n + lon] = back[chunk, :, here]

    def finish(chunk):
        @pl.loop(0, lon_n)
        def _(k):
            @pl.when(k > 0)
            def _():
                send_back(chunk, k).wait_recv()

            pos = source(k)
            row = row_at(chunk, pos)
            mixed = jnp.dot(mix_t[...], spatial[chunk * lon_n + pos], preferred_element_type=F32)
            wet_row = mask_ref[pl.ds(row, 1), :].astype(F32)
            val = wet_row * (res[row].astype(F32) + mixed)
            flat[0, pl.ds(row, padded, stride=rows), :] = val[:, :LANES]
            flat[1, pl.ds(row, padded, stride=rows), :] = val[:, LANES:]

    halo_done = False
    for chunk in range(per):
        out_rows = [(chunk * lon_n + q + HALO) % rows for q in range(lon_n)]
        if not halo_done and (min(out_rows) < HALO or max(out_rows) >= rows - HALO):
            await_halo()
            halo_done = True
        conv(out_rows)
        mix_rows(chunk)
        if chunk == 1:
            table_copy.wait()
            spec_copy.wait()
        if chunk >= 1:
            spectral(chunk - 1)
    if per == 1:
        table_copy.wait()
        spec_copy.wait()
    for chunk in range(per - 2):
        finish(chunk)
    spectral(per - 1)
    for chunk in range(max(per - 2, 0), per):
        finish(chunk)

    @pl.loop(0, channels)
    def _(c):
        at = pl.multiple_of(c * rows, rows)
        out_ref[c, :, :LANES] = flat[0, pl.ds(at, rows), :].astype(BF16)
        out_ref[c, :, LANES:] = flat[1, pl.ds(at, rows), :].astype(BF16)

    for chunk in range(per):
        for k in range(lon_n - 1, 0, -1):
            send_row(chunk, k).wait_send()
            send_back(chunk, k).wait_send()


def local(lat_n, lon_n, field, land_mask, fold_partner, dw_kernel, norm_gain, w_in, w_out, spec_gain, mix_weight):
    channels, rows, cols = field.shape
    modes = spec_gain.shape[2]
    hid = w_in.shape[1]
    lon_points = cols * lon_n
    padded = -(-channels // 16) * 16
    hid_up = -(-hid // 16) * 16
    table = jnp.asarray(dft_table(lon_points, modes))
    taps = dw_kernel.transpose(1, 2, 0)
    per = rows // lon_n
    sizes = (channels, padded, rows, cols, lat_n, lon_n, modes)
    vmem = pl.BlockSpec(memory_space=pltpu.VMEM)
    hbm = pl.BlockSpec(memory_space=pl.ANY)
    dma = pltpu.SemaphoreType.DMA
    peers = lon_n - 1
    return pl.pallas_call(
        functools.partial(kernel, sizes),
        out_shape=jax.ShapeDtypeStruct(field.shape, BF16),
        in_specs=[vmem] * 8 + [hbm] * 2,
        out_specs=vmem,
        scratch_shapes=[
            pltpu.VMEM((2, padded * rows, LANES), F32),
            pltpu.VMEM((rows + 2 * HALO, padded, cols + LANES), F32),
            pltpu.VMEM((rows, padded, cols), BF16),
            pltpu.VMEM((rows, padded, cols), F32),
            pltpu.VMEM((rows, padded, cols), BF16),
            pltpu.VMEM((per, padded, lon_points), BF16),
            pltpu.VMEM((per, padded, lon_points), BF16),
            pltpu.VMEM((rows, padded, cols), BF16),
            *[pltpu.VMEM((padded, LANES), BF16)] * 6,
            *[pltpu.VMEM((HALO, padded, cols), BF16)] * 2,
            pltpu.VMEM((HALO, padded, lon_points), BF16),
            pltpu.VMEM(spec_gain.shape, F32),
            pltpu.VMEM(table.shape, BF16),
            pltpu.VMEM((TAPS * TAPS, padded, LANES), F32),
            pltpu.VMEM((hid_up, padded), BF16),
            pltpu.VMEM((padded, hid_up), BF16),
            pltpu.VMEM((padded, padded), BF16),
            pltpu.VMEM((padded, LANES), F32),
            *[dma((2,))] * 7,
            *[dma((peers,))] * 2,
            *[dma((peers * per,))] * 4,
        ],
        compiler_params=pltpu.CompilerParams(
            collective_id=0, has_side_effects=True, vmem_limit_bytes=62 * 1024 * 1024),
        name="block",
    )(field, land_mask, fold_partner[None, :], taps, norm_gain[None, :], w_in, w_out.T, mix_weight, spec_gain, table)


def solution(mesh):
    placed = (P(None, "lat", "lon"), P("lat", "lon"), P(), P(), P(), P(), P(), P(), P())
    return jax.shard_map(
        functools.partial(local, mesh.shape["lat"], mesh.shape["lon"]),
        mesh=mesh, in_specs=placed, out_specs=P(None, "lat", "lon"), check_vma=False,
    )
```

profile of v0, /device:TPU:0, one launch (start us, length us, event | category | flops | bytes accessed | tf_op | source)
XLA Modules:
  0.0 58.5 jit_solution(9388470326375301727)
XLA Ops:
  0.0 2.0 %copy.11.spec_hbm = f32[2,150,512]{2,1,0:T(8,128)} copy(f32[2,150,512]{2,0,1:T(2,128)} %param.17) | data formatting | bytes 1228800 | tf_op args[7]
  2.0 54.1 %block.1 = bf16[150,16,256]{2,1,0:T(8,128)(2,1)} custom-call(bf16[150,16,256]{2,1,0:T(8,128)(2,1)} %field_ref.1, s32[16,256]{1,0:T(8,128)} %mask_ref.1, s32[1,1024]{1,0:T(1,128)} %bitcast.6, f32[7,7,150]{2,1,0:T(8,128)} %bitcast.5, f32[1,150]{1,0:T(1,128)} %bitcast.7, bf16[150,600]{1,0:T(8,128)(2,1)} %w_in_ref.1, bf16[150,600]{1,0:T(8,128)(2,1)} %bitcast.4, ...), custom_call_target="tpu_custom_call" | custom-call | tf_op jit(solution)/shard_map/block/pallas_call | solution.py:376
  56.1 2.4 %copy.13 = bf16[150,16,256]{2,1,0:T(8,128)(2,1)} copy(bf16[150,16,256]{2,1,0:T(8,128)(2,1)} %block.1) | data formatting | bytes 2457600
where the time goes:
time: 58.7 us; the launch traced here: 58.5 us
  Pallas kernels  54.1 us (92%)
  local copies, waits for them, and re-layouts  4.42 us (8%)
    pallas_call x1, Pallas kernels, local(): pl.pallas_call(functools.partial(kernel, sizes), out_shape=jax.ShapeDtype...  54.1 us
    unnamed x2, local copies, waits for them, and re-layouts  4.42 us

commit v1 on v0

v1 whole, which is shorter than its diff:
```python
import functools
import math

import jax
import jax.numpy as jnp
import numpy as np
from jax import lax
from jax.experimental import pallas as pl
from jax.experimental.pallas import tpu as pltpu
from jax.sharding import PartitionSpec as P

F32 = jnp.float32
BF16 = jnp.bfloat16
TAPS = 7
HALO = 3
LANES = 128
WORK = BF16
VMEM_LIMIT = 58 * 1024 * 1024


def dft_table(lon_points, mode_count):
    phase = np.arange(lon_points)[:, None] * np.arange(mode_count)[None, :] % lon_points
    angles = phase.astype(np.float32) * np.float32(2.0 * math.pi / lon_points)
    factor = np.float32(1.0 / math.sqrt(lon_points))
    angles = angles.astype(np.float64)
    table = np.concatenate([np.cos(angles), -np.sin(angles)], axis=1).astype(np.float32)
    return (table * factor).astype(BF16)


def kernel(
    sizes,
    field_hbm, mask_hbm, fold_hbm, taps_hbm, gain_hbm, w_in_hbm, w_out_hbm, mix_hbm, spec_hbm, table_hbm,
    out_ref,
    field_ref, mask_ref, fold_ref, taps_ref, gain_ref, w_in_ref, w_out_ref, mix_ref, spec_raw, table_ref,
    flat, own, depth, flat_out, halo, toep, pattern_t, pattern, pattern_back, edge32, comb32,
    res, by_rows, back, spatial,
    edge_mine, edge_left, edge_right, comb, comb_n, comb_s, rows_n, rows_s, top_all,
    spec_ref, w_in_t, w_out_t, mix_t, gain_col,
    local_sem, edge_send, edge_recv, comb_send, comb_recv, rows_send, rows_recv,
    fold_send, fold_recv, out_send, out_recv, in_send, in_recv,
):
    channels, rows, cols, lat_n, lon_n, modes = sizes
    lon_points = cols * lon_n
    tiles = cols // LANES
    per = rows // lon_n
    step = max(u for u in range(1, 11) if channels % u == 0)
    lat = lax.axis_index("lat")
    lon = lax.axis_index("lon")
    left = lax.rem(lon + lon_n - 1, lon_n)
    right = lax.rem(lon + 1, lon_n)
    chip = lon // 2
    core = lax.rem(lon, 2)
    chips = lon_n // 2
    mate_core = chip * 2 + 1 - core

    def target(k):
        return lax.rem(chip + k // 2, chips) * 2 + lax.rem(core + lax.rem(k, 2), 2)

    def source(k):
        return lax.rem(chip + chips - k // 2, chips) * 2 + lax.rem(core + lax.rem(k, 2), 2)

    pairs = (
        (mask_hbm, mask_ref), (field_hbm, field_ref), (taps_hbm, taps_ref), (fold_hbm, fold_ref), (gain_hbm, gain_ref),
        (w_in_hbm, w_in_ref), (w_out_hbm, w_out_ref), (mix_hbm, mix_ref), (spec_hbm, spec_raw), (table_hbm, table_ref))
    loads = [pltpu.make_async_copy(a, b, local_sem.at[n]) for n, (a, b) in enumerate(pairs)]
    loads[0].start()
    loads[1].start()

    barrier = pltpu.get_barrier_semaphore()
    for k in range(1, lon_n):
        pl.semaphore_signal(barrier, inc=1, device_id={"lon": target(k)})

    @pl.when(lat > 0)
    def _():
        pl.semaphore_signal(barrier, inc=1, device_id={"lat": lat - 1})

    @pl.when(lat < lat_n - 1)
    def _():
        pl.semaphore_signal(barrier, inc=1, device_id={"lat": lat + 1})

    for load in loads[2:]:
        load.start()

    lane = lax.broadcasted_iota(jnp.int32, (rows, LANES), 1)
    loads[0].wait()
    loads[1].wait()
    wet = mask_ref[...].astype(F32)

    @pl.loop(0, channels // step)
    def _(group):
        for u in range(step):
            c = group * step + u
            val = field_ref[c].astype(F32) * wet
            at = pl.multiple_of(c * rows, rows)
            parts = [val[:, h * LANES : (h + 1) * LANES] for h in range(tiles)]
            for h in range(tiles):
                flat[h, pl.ds(at, rows), :] = parts[h]
            edge = jnp.where(lane < HALO, parts[0], jnp.where(lane >= LANES - HALO, parts[-1], 0.0))
            edge = pltpu.roll(edge, 0, 1, stride=8, stride_axis=0)
            edge32[pl.ds(c, 1), :] = jnp.sum(edge, axis=0, keepdims=True)

    edge_mine[...] = edge32[...].astype(BF16)

    count = lon_n - 1 + jnp.where(lat > 0, 1, 0) + jnp.where(lat < lat_n - 1, 1, 0)
    pl.semaphore_wait(barrier, count)

    to_left = pltpu.make_async_remote_copy(
        edge_mine, edge_right, edge_send.at[0], edge_recv.at[0], device_id={"lon": left})
    to_right = pltpu.make_async_remote_copy(
        edge_mine, edge_left, edge_send.at[1], edge_recv.at[1], device_id={"lon": right})
    to_left.start()
    to_right.start()

    def own_row(i):
        for h in range(tiles):
            own[i, :, h * LANES : (h + 1) * LANES] = flat[h, pl.ds(i, channels, stride=rows), :].astype(BF16)

    rows_down = pltpu.make_async_remote_copy(
        own.at[pl.ds(0, HALO)], rows_n, rows_send.at[0], rows_recv.at[0], device_id={"lat": lat - 1})
    rows_up = pltpu.make_async_remote_copy(
        own.at[pl.ds(rows - HALO, HALO)], rows_s, rows_send.at[1], rows_recv.at[1], device_id={"lat": lat + 1})
    comb_down = pltpu.make_async_remote_copy(
        comb, comb_n, comb_send.at[0], comb_recv.at[0], device_id={"lat": lat - 1})
    comb_up = pltpu.make_async_remote_copy(
        comb, comb_s, comb_send.at[1], comb_recv.at[1], device_id={"lat": lat + 1})

    def piece(pos):
        return top_all.at[:, :, pl.ds(pl.multiple_of(pos * cols, LANES), cols)]

    def fold_out(j):
        whom = mate_core if j == 0 else lax.rem(chip + j, chips) * 2 + core
        return pltpu.make_async_remote_copy(
            own.at[pl.ds(rows - HALO, HALO)], piece(lon), fold_send.at[j], fold_recv.at[j], device_id={"lon": whom})

    def fold_pass(j):
        pos = lax.rem(chip + chips - j, chips) * 2 + core
        return pltpu.make_async_remote_copy(
            piece(pos), piece(pos), fold_send.at[chips + j - 1], fold_recv.at[chips + j - 1], device_id={"lon": mate_core})

    for i in range(rows - HALO, rows):
        own_row(i)

    @pl.when(lat < lat_n - 1)
    def _():
        rows_up.start()

    @pl.when(lat == lat_n - 1)
    def _():
        for j in range(chips - 1, -1, -1):
            fold_out(j).start()
        top_all[:, :, pl.ds(pl.multiple_of(lon * cols, LANES), cols)] = own[rows - HALO :]

    for i in range(HALO):
        own_row(i)

    @pl.when(lat > 0)
    def _():
        rows_down.start()

    loads[2].wait()
    pattern_t[...] = jnp.zeros(pattern_t.shape, F32)
    for a in range(TAPS):
        for b in range(TAPS):
            pattern_t[b * rows + a : b * rows + a + 1, :channels] = taps_ref[a, b : b + 1, :]
    pattern[...] = pattern_t[...].T[:channels]
    pattern_back[...] = pltpu.roll(pattern[...], LANES - HALO, 1)

    slot = lax.rem(lane, rows)
    index = lax.broadcasted_iota(jnp.int32, (rows, LANES), 0)
    band = jnp.abs(slot - index) <= HALO
    half = rows // 2
    low_slot = slot[:half] < HALO
    high_slot = (slot[:half] >= half + HALO) & (slot[:half] < half + 2 * HALO)

    @pl.loop(0, channels // step)
    def _(group):
        for u in range(step):
            c = group * step + u
            row = jnp.broadcast_to(pattern_back[pl.ds(c, 1), :], (rows, LANES))
            mid = jnp.where(band, pltpu.roll(row, 0, 1, stride=1, stride_axis=0), 0.0)
            row = jnp.broadcast_to(pattern[pl.ds(c, 1), :], (half, LANES))
            far = pltpu.roll(row, 0, 1, stride=1, stride_axis=0)
            far = jnp.concatenate([jnp.where(low_slot, far, 0.0), jnp.where(high_slot, far, 0.0)], axis=0)
            for n, part in enumerate((mid, far)):
                coarse = part.astype(BF16)
                toep[c, 2 * n * rows : (2 * n + 1) * rows, :] = coarse
                toep[c, (2 * n + 1) * rows : (2 * n + 2) * rows, :] = (part - coarse.astype(F32)).astype(BF16)

    halo[...] = jnp.zeros(halo.shape, F32)

    for i in range(HALO, rows - HALO):
        own_row(i)

    def turned(ref, target_ref):
        n, m = ref.shape
        up = [-(-d // LANES) * LANES for d in (n, m)]
        full = jnp.concatenate([ref[...].astype(F32), jnp.zeros((n, up[1] - m), F32)], axis=1)
        full = jnp.concatenate([full, jnp.zeros((up[0] - n, up[1]), F32)], axis=0)
        target_ref[...] = full.T[: target_ref.shape[0], : target_ref.shape[1]].astype(BF16)

    to_left.wait()
    to_right.wait()
    near = lax.rem(lax.broadcasted_iota(jnp.int32, (channels, LANES), 1), 8) < 4
    both = jnp.where(near, edge_right[...].astype(F32), edge_left[...].astype(F32))
    comb[...] = both.astype(BF16)
    comb32[...] = both

    @pl.when(lat > 0)
    def _():
        comb_down.start()

    @pl.when(lat < lat_n - 1)
    def _():
        comb_up.start()

    def shifted(ring):
        blocks = []
        for b in range(TAPS):
            d = b - HALO
            line = []
            for h in range(tiles):
                if d == 0:
                    line.append(ring[h])
                elif d > 0:
                    line.append(pltpu.roll(jnp.where(lane < d, ring[h + 1], ring[h]), LANES - d, 1))
                else:
                    line.append(pltpu.roll(jnp.where(lane >= LANES + d, ring[h - 1], ring[h]), -d, 1))
            blocks.append(jnp.concatenate(line, axis=1).astype(BF16))
        return jnp.concatenate(blocks, axis=0)

    def product(c, which, ring):
        weights = toep[c, 2 * which * rows : 2 * (which + 1) * rows, : TAPS * rows]
        total = jnp.dot(weights, shifted(ring), preferred_element_type=F32)
        return total[:rows] + total[rows:]

    @pl.loop(0, channels // step)
    def _(group):
        for u in range(step):
            c = group * step + u
            rim = jnp.broadcast_to(comb32[pl.ds(c, 1), :], (half, LANES))
            for bit in (1, 2, 4):
                rim = jnp.where(lax.rem(index[:half] // bit, 2) == 1, pltpu.roll(rim, LANES - 8 * bit, 1), rim)
            rim = jnp.concatenate([rim, pltpu.roll(rim, LANES - 8 * half, 1)], axis=0)
            at = pl.multiple_of(c * rows, rows)
            ring = [flat[h, pl.ds(at, rows), :].astype(WORK) for h in range(tiles)] + [rim.astype(WORK)]
            total = product(c, 0, ring)
            for h in range(tiles):
                depth[h, pl.ds(at, rows), :] = total[:, h * LANES : (h + 1) * LANES]

    for n in range(5, 8):
        loads[n].wait()
    loads[4].wait()
    turned(w_in_ref, w_in_t)
    w_out_t[...] = jnp.zeros(w_out_t.shape, BF16)
    w_out_t[:, : w_out_ref.shape[1]] = w_out_ref[...]
    turned(mix_ref, mix_t)
    diagonal = lax.broadcasted_iota(jnp.int32, (channels, channels), 0) == lax.broadcasted_iota(
        jnp.int32, (channels, channels), 1)
    gain_col[...] = jnp.broadcast_to(
        jnp.sum(jnp.where(diagonal, gain_ref[...], 0.0), axis=1, keepdims=True), (channels, LANES))

    def edges_of(packed, i):
        return pltpu.roll(packed, LANES - 8 * i, 1) if i else packed

    def put_halo(at, value, rim):
        for h in range(tiles):
            halo[h, pl.ds(at, channels, stride=half), :] = value[:, h * LANES : (h + 1) * LANES]
        halo[tiles, pl.ds(at, channels, stride=half), :] = rim

    def await_halo():
        loads[3].wait()

        @pl.when(lat > 0)
        def _():
            rows_down.wait_send()
            comb_down.wait_send()
            rows_up.wait_recv()
            comb_up.wait_recv()
            for r in range(HALO):
                put_halo(r, rows_s[r].astype(F32), edges_of(comb_s[...].astype(F32), rows - HALO + r))

        @pl.when(lat < lat_n - 1)
        def _():
            rows_up.wait_send()
            comb_up.wait_send()
            rows_down.wait_recv()
            comb_down.wait_recv()
            for r in range(HALO):
                put_halo(HALO + r, rows_n[r].astype(F32), edges_of(comb_n[...].astype(F32), r))

        @pl.when(lat == lat_n - 1)
        def _():
            for j in range(1, chips):
                fold_out(j).wait_recv()
                fold_pass(j).start()
            for j in range(chips):
                fold_out(j).wait_send()
            fold_out(0).wait_recv()
            for j in range(1, chips):
                fold_pass(j).wait()
            point = lax.broadcasted_iota(jnp.int32, (lon_points, cols + LANES), 0)
            at = lax.broadcasted_iota(jnp.int32, (1, cols + LANES), 1)
            at = jnp.where(at < cols + HALO, at, at - (cols + LANES)) + lon * cols
            mate = fold_ref[:, :1] - at
            mate = jnp.where(mate < 0, mate + lon_points, mate)
            mate = jnp.where(mate < 0, mate + lon_points, mate)
            mate = jnp.where(mate >= lon_points, mate - lon_points, mate)
            pick = jnp.where(point == mate, 1.0, 0.0).astype(BF16)
            for r in range(HALO):
                row = jnp.dot(top_all[HALO - 1 - r], pick, preferred_element_type=F32)
                put_halo(HALO + r, row[:, :cols], row[:, cols:])

        @pl.loop(0, channels // step)
        def _(group):
            for u in range(step):
                c = group * step + u
                spot = pl.ds(pl.multiple_of(c * half, half), half)
                ring = [jnp.concatenate([halo[h, spot, :]] * 2, axis=0).astype(WORK) for h in range(tiles + 1)]
                total = product(c, 1, ring)
                at = pl.multiple_of(c * rows, rows)
                for h in range(tiles):
                    depth[h, pl.ds(at, rows), :] += total[:, h * LANES : (h + 1) * LANES]

    here = pl.ds(pl.multiple_of(lon * cols, LANES), cols)

    def row_at(chunk, q):
        return lax.rem(chunk * lon_n + q + HALO, rows)

    def send_row(chunk, k):
        s = chunk * (lon_n - 1) + lon_n - 1 - k
        return pltpu.make_async_remote_copy(
            res.at[row_at(chunk, target(k))], by_rows.at[chunk, :, here],
            out_send.at[s], out_recv.at[s], device_id={"lon": target(k)})

    def send_back(chunk, k):
        q = target(k)
        s = chunk * (lon_n - 1) + lon_n - 1 - k
        return pltpu.make_async_remote_copy(
            back.at[chunk, :, pl.ds(pl.multiple_of(q * cols, LANES), cols)], spatial.at[chunk * lon_n + lon],
            in_send.at[s], in_recv.at[s], device_id={"lon": q})

    def mix_rows(chunk):
        @pl.loop(0, lon_n // 2)
        def _(pair):
            k = lon_n - 1 - 2 * pair
            one, two = row_at(chunk, target(k)), row_at(chunk, target(k - 1))
            x = jnp.concatenate(
                [depth[h, pl.ds(row, channels, stride=rows), :] for row in (one, two) for h in range(tiles)], axis=1)
            mean = jnp.sum(x, axis=0, keepdims=True) * (1.0 / channels)
            centred = x - mean
            var = jnp.sum(centred * centred, axis=0, keepdims=True) * (1.0 / channels)
            gain = jnp.concatenate([gain_col[...]] * (2 * tiles), axis=1)
            normed = (centred * lax.rsqrt(var + 1e-06) * gain).astype(BF16)
            pre = jnp.dot(w_in_t[...], normed, preferred_element_type=F32)
            hidden = jax.nn.gelu(pre, approximate=True).astype(BF16)
            branch = jnp.dot(w_out_t[...], hidden, preferred_element_type=F32)
            for n, row in enumerate((one, two)):
                wet_row = mask_ref[pl.ds(row, 1), :].astype(F32)
                part = branch[:, n * cols : (n + 1) * cols]
                res[row] = (wet_row * (own[row].astype(F32) + part)).astype(BF16)
            send_row(chunk, k).start()

            @pl.when(pair < lon_n // 2 - 1)
            def _():
                send_row(chunk, k - 1).start()

            @pl.when(pair == lon_n // 2 - 1)
            def _():
                by_rows[chunk, :, here] = res[two]

    def spectral(chunk):
        for k in range(lon_n - 1, 0, -1):
            send_row(chunk, k).wait_recv()
        spectrum = jnp.dot(by_rows[chunk], table_ref[...], preferred_element_type=F32)
        s_re = spectrum[:, :modes]
        s_im = spectrum[:, modes:]
        g_re = spec_ref[0]
        g_im = spec_ref[1]
        scaled = jnp.concatenate(
            [(g_re * s_re - g_im * s_im).astype(BF16), (g_re * s_im + g_im * s_re).astype(BF16)], axis=1)
        back[chunk] = lax.dot_general(
            scaled, table_ref[...], (((1,), (1,)), ((), ())), preferred_element_type=F32).astype(BF16)
        for k in range(lon_n - 1, 0, -1):
            send_back(chunk, k).start()
        spatial[chunk * lon_n + lon] = back[chunk, :, here]

    def finish(chunk):
        @pl.loop(0, lon_n)
        def _(k):
            @pl.when(k > 0)
            def _():
                send_back(chunk, k).wait_recv()

            pos = source(k)
            row = row_at(chunk, pos)
            mixed = jnp.dot(mix_t[...], spatial[chunk * lon_n + pos], preferred_element_type=F32)
            wet_row = mask_ref[pl.ds(row, 1), :].astype(F32)
            val = wet_row * (res[row].astype(F32) + mixed)
            for h in range(tiles):
                flat_out[h, pl.ds(row, channels, stride=rows), :] = val[:, h * LANES : (h + 1) * LANES]

    halo_done = False
    for chunk in range(per):
        out_rows = [(chunk * lon_n + q + HALO) % rows for q in range(lon_n)]
        if not halo_done and (min(out_rows) < HALO or max(out_rows) >= rows - HALO):
            await_halo()
            halo_done = True
        mix_rows(chunk)

    loads[8].wait()
    wide = modes // LANES
    for p in range(2):
        for t in range(wide):
            spec_ref[p, :, t * LANES : (t + 1) * LANES] = spec_raw[pl.ds(2 * t + p, channels, stride=2 * wide), :]
    loads[9].wait()

    for chunk in range(per):
        spectral(chunk)
    for chunk in range(per):
        finish(chunk)

    @pl.loop(0, channels // step)
    def _(group):
        for u in range(step):
            c = group * step + u
            at = pl.multiple_of(c * rows, rows)
            for h in range(tiles):
                out_ref[c, :, h * LANES : (h + 1) * LANES] = flat_out[h, pl.ds(at, rows), :].astype(BF16)

    for chunk in range(per):
        for k in range(lon_n - 1, 0, -1):
            send_row(chunk, k).wait_send()
            send_back(chunk, k).wait_send()


def local(lat_n, lon_n, field, land_mask, fold_partner, dw_kernel, norm_gain, w_in, w_out, spec_gain, mix_weight):
    channels, rows, cols = field.shape
    modes = spec_gain.shape[2]
    hid = w_in.shape[1]
    lon_points = cols * lon_n
    hid_up = -(-hid // 16) * 16
    chan_up = -(-channels // LANES) * LANES
    tiles = cols // LANES
    table = jnp.asarray(dft_table(lon_points, modes))
    taps = dw_kernel.transpose(1, 2, 0)
    wide = modes // LANES
    spec = spec_gain.transpose(1, 0, 2).reshape(channels, 2, wide, LANES).transpose(0, 2, 1, 3).reshape(-1, LANES)
    per = rows // lon_n
    sizes = (channels, rows, cols, lat_n, lon_n, modes)
    operands = (field, land_mask, fold_partner[None, :], taps, norm_gain[None, :], w_in, w_out.T, mix_weight, spec, table)
    dma = pltpu.SemaphoreType.DMA
    peers = lon_n - 1
    return pl.pallas_call(
        functools.partial(kernel, sizes),
        out_shape=jax.ShapeDtypeStruct(field.shape, BF16),
        in_specs=[pl.BlockSpec(memory_space=pltpu.HBM)] * len(operands),
        out_specs=pl.BlockSpec(memory_space=pltpu.VMEM),
        scratch_shapes=[
            *[pltpu.VMEM(x.shape, x.dtype) for x in operands],
            pltpu.VMEM((tiles, channels * rows, LANES), F32),
            pltpu.VMEM((rows, channels, cols), BF16),
            pltpu.VMEM((tiles, channels * rows, LANES), F32),
            pltpu.VMEM((tiles, channels * rows, LANES), F32),
            pltpu.VMEM((tiles + 1, channels * rows // 2, LANES), F32),
            pltpu.VMEM((channels, 4 * rows, LANES), BF16),
            pltpu.VMEM((LANES, chan_up), F32),
            *[pltpu.VMEM((channels, LANES), F32)] * 4,
            pltpu.VMEM((rows, channels, cols), BF16),
            pltpu.VMEM((per, channels, lon_points), BF16),
            pltpu.VMEM((per, channels, lon_points), BF16),
            pltpu.VMEM((rows, channels, cols), BF16),
            *[pltpu.VMEM((channels, LANES), BF16)] * 6,
            *[pltpu.VMEM((HALO, channels, cols), BF16)] * 2,
            pltpu.VMEM((HALO, channels, lon_points), BF16),
            pltpu.VMEM(spec_gain.shape, F32),
            pltpu.VMEM((hid_up, channels), BF16),
            pltpu.VMEM((channels, hid_up), BF16),
            pltpu.VMEM((channels, channels), BF16),
            pltpu.VMEM((channels, LANES), F32),
            dma((len(operands),)),
            *[dma((2,))] * 6,
            *[dma((peers,))] * 2,
            *[dma((peers * per,))] * 4,
        ],
        compiler_params=pltpu.CompilerParams(
            collective_id=0, has_side_effects=True, vmem_limit_bytes=VMEM_LIMIT),
        name="block",
    )(*operands)


def solution(mesh):
    placed = (P(None, "lat", "lon"), P("lat", "lon"), P(), P(), P(), P(), P(), P(), P())
    return jax.shard_map(
        functools.partial(local, mesh.shape["lat"], mesh.shape["lon"]),
        mesh=mesh, in_specs=placed, out_specs=P(None, "lat", "lon"), check_vma=False,
    )
```

time: 58.7 us -> 54.3 us (0.925)
  the two profiles are of different devices: /device:TPU:0 before, /device:TPU:28 now
where the time goes in v1:
time: 54.3 us; the launch traced here: 54.1 us
  Pallas kernels  51.7 us (95%)
  local copies, waits for them, and re-layouts  2.4 us (4%)
    pallas_call x1, Pallas kernels, local(): pl.pallas_call(functools.partial(kernel, sizes), out_shape=jax.ShapeDtype...  51.7 us
    unnamed x1, local copies, waits for them, and re-layouts  2.4 us

profile of v1, /device:TPU:28, one launch (start us, length us, event | category | flops | bytes accessed | tf_op | source)
XLA Modules:
  0.0 54.1 jit_solution(6570695238920118212)
XLA Ops:
  0.0 51.7 %block.1 = bf16[150,16,256]{2,1,0:T(8,128)(2,1)} custom-call(bf16[150,16,256]{2,1,0:T(8,128)(2,1)} %field_hbm.1, s32[16,256]{1,0:T(8,128)} %mask_hbm.1, s32[1,1024]{1,0:T(1,128)} %bitcast.14, f32[7,7,150]{2,1,0:T(8,128)} %bitcast.13, f32[1,150]{1,0:T(1,128)} %bitcast.15, bf16[150,600]{1,0:T(8,128)(2,1)} %w_in_hbm.1, bf16[150,600]{1,0:T(8,128)(2,1)} %bitcast.12, ...), custom_call_target="tpu_custom_call" | custom-call | tf_op jit(solution)/shard_map/block/pallas_call | solution.py:453
  51.7 2.4 %copy.13 = bf16[150,16,256]{2,1,0:T(8,128)(2,1)} copy(bf16[150,16,256]{2,1,0:T(8,128)(2,1)} %block.1) | data formatting | bytes 2457600

commit v2 on v1

--- a/solution.py
+++ b/solution.py
@@ -15,6 +15,7 @@
 HALO = 3
 LANES = 128
 WORK = BF16
+STEP = 30
 VMEM_LIMIT = 58 * 1024 * 1024
 
 
@@ -43,7 +44,7 @@
     lon_points = cols * lon_n
     tiles = cols // LANES
     per = rows // lon_n
-    step = max(u for u in range(1, 11) if channels % u == 0)
+    step = max(u for u in range(2, STEP + 1, 2) if channels % u == 0)
     lat = lax.axis_index("lat")
     lon = lax.axis_index("lon")
     left = lax.rem(lon + lon_n - 1, lon_n)
@@ -59,12 +60,20 @@
     def source(k):
         return lax.rem(chip + chips - k // 2, chips) * 2 + lax.rem(core + lax.rem(k, 2), 2)
 
-    pairs = (
-        (mask_hbm, mask_ref), (field_hbm, field_ref), (taps_hbm, taps_ref), (fold_hbm, fold_ref), (gain_hbm, gain_ref),
-        (w_in_hbm, w_in_ref), (w_out_hbm, w_out_ref), (mix_hbm, mix_ref), (spec_hbm, spec_raw), (table_hbm, table_ref))
-    loads = [pltpu.make_async_copy(a, b, local_sem.at[n]) for n, (a, b) in enumerate(pairs)]
+    whole = (
+        (taps_hbm, taps_ref), (mask_hbm, mask_ref), (fold_hbm, fold_ref), (gain_hbm, gain_ref), (w_in_hbm, w_in_ref),
+        (w_out_hbm, w_out_ref), (mix_hbm, mix_ref), (spec_hbm, spec_raw), (table_hbm, table_ref))
+    loads = [pltpu.make_async_copy(a, b, local_sem.at[n]) for n, (a, b) in enumerate(whole)]
+    groups = channels // step
+
+    def field_load(group):
+        some = pl.ds(group * step, step)
+        return pltpu.make_async_copy(field_hbm.at[some], field_ref.at[some], local_sem.at[len(whole) + group])
+
     loads[0].start()
     loads[1].start()
+    for group in range(groups):
+        field_load(group).start()
 
     barrier = pltpu.get_barrier_semaphore()
     for k in range(1, lon_n):
@@ -82,7 +91,6 @@
         load.start()
 
     lane = lax.broadcasted_iota(jnp.int32, (rows, LANES), 1)
-    loads[0].wait()
     loads[1].wait()
     wet = mask_ref[...].astype(F32)
 
@@ -90,6 +98,8 @@
     def _(group):
         for u in range(step):
             c = group * step + u
+            if u == 0:
+                field_load(group).wait()
             val = field_ref[c].astype(F32) * wet
             at = pl.multiple_of(c * rows, rows)
             parts = [val[:, h * LANES : (h + 1) * LANES] for h in range(tiles)]
@@ -157,7 +167,7 @@
     def _():
         rows_down.start()
 
-    loads[2].wait()
+    loads[0].wait()
     pattern_t[...] = jnp.zeros(pattern_t.shape, F32)
     for a in range(TAPS):
         for b in range(TAPS):
@@ -188,9 +198,6 @@
 
     halo[...] = jnp.zeros(halo.shape, F32)
 
-    for i in range(HALO, rows - HALO):
-        own_row(i)
-
     def turned(ref, target_ref):
         n, m = ref.shape
         up = [-(-d // LANES) * LANES for d in (n, m)]
@@ -198,6 +205,20 @@
         full = jnp.concatenate([full, jnp.zeros((up[0] - n, up[1]), F32)], axis=0)
         target_ref[...] = full.T[: target_ref.shape[0], : target_ref.shape[1]].astype(BF16)
 
+    for n in range(3, 7):
+        loads[n].wait()
+    turned(w_in_ref, w_in_t)
+    w_out_t[...] = jnp.zeros(w_out_t.shape, BF16)
+    w_out_t[:, : w_out_ref.shape[1]] = w_out_ref[...]
+    turned(mix_ref, mix_t)
+    diagonal = lax.broadcasted_iota(jnp.int32, (channels, channels), 0) == lax.broadcasted_iota(
+        jnp.int32, (channels, channels), 1)
+    gain_col[...] = jnp.broadcast_to(
+        jnp.sum(jnp.where(diagonal, gain_ref[...], 0.0), axis=1, keepdims=True), (channels, LANES))
+
+    for i in range(HALO, rows - HALO):
+        own_row(i)
+
     to_left.wait()
     to_right.wait()
     near = lax.rem(lax.broadcasted_iota(jnp.int32, (channels, LANES), 1), 8) < 4
@@ -213,7 +234,9 @@
     def _():
         comb_up.start()
 
-    def shifted(ring):
+    def shifted(ring, finish_block):
+        high = ring[0].shape[0]
+        at = lane[:high]
         blocks = []
         for b in range(TAPS):
             d = b - HALO
@@ -222,42 +245,39 @@
                 if d == 0:
                     line.append(ring[h])
                 elif d > 0:
-                    line.append(pltpu.roll(jnp.where(lane < d, ring[h + 1], ring[h]), LANES - d, 1))
+                    line.append(pltpu.roll(jnp.where(at < d, ring[h + 1], ring[h]), LANES - d, 1))
                 else:
-                    line.append(pltpu.roll(jnp.where(lane >= LANES + d, ring[h - 1], ring[h]), -d, 1))
-            blocks.append(jnp.concatenate(line, axis=1).astype(BF16))
-        return jnp.concatenate(blocks, axis=0)
-
-    def product(c, which, ring):
-        weights = toep[c, 2 * which * rows : 2 * (which + 1) * rows, : TAPS * rows]
-        total = jnp.dot(weights, shifted(ring), preferred_element_type=F32)
-        return total[:rows] + total[rows:]
+                    line.append(pltpu.roll(jnp.where(at >= LANES + d, ring[h - 1], ring[h]), -d, 1))
+            blocks.append(finish_block(jnp.concatenate(line, axis=1)))
+        return jnp.concatenate(blocks + [blocks[-1]] * (LANES // rows - TAPS), axis=0)
+
+    blank = jnp.zeros((2 * rows, LANES), BF16)
+
+    def product(c, which, rings, finish_block):
+        span = slice(2 * which * rows, 2 * (which + 1) * rows)
+        weights = jnp.concatenate(
+            [jnp.concatenate([toep[c, span, :], blank], axis=1), jnp.concatenate([blank, toep[c + 1, span, :]], axis=1)],
+            axis=0)
+        points = jnp.concatenate([shifted(ring, finish_block) for ring in rings], axis=0)
+        total = jnp.dot(weights, points, preferred_element_type=F32)
+        return total[:rows] + total[rows : 2 * rows], total[2 * rows : 3 * rows] + total[3 * rows :]
 
     @pl.loop(0, channels // step)
     def _(group):
-        for u in range(step):
-            c = group * step + u
-            rim = jnp.broadcast_to(comb32[pl.ds(c, 1), :], (half, LANES))
-            for bit in (1, 2, 4):
-                rim = jnp.where(lax.rem(index[:half] // bit, 2) == 1, pltpu.roll(rim, LANES - 8 * bit, 1), rim)
-            rim = jnp.concatenate([rim, pltpu.roll(rim, LANES - 8 * half, 1)], axis=0)
-            at = pl.multiple_of(c * rows, rows)
-            ring = [flat[h, pl.ds(at, rows), :].astype(WORK) for h in range(tiles)] + [rim.astype(WORK)]
-            total = product(c, 0, ring)
-            for h in range(tiles):
-                depth[h, pl.ds(at, rows), :] = total[:, h * LANES : (h + 1) * LANES]
-
-    for n in range(5, 8):
-        loads[n].wait()
-    loads[4].wait()
-    turned(w_in_ref, w_in_t)
-    w_out_t[...] = jnp.zeros(w_out_t.shape, BF16)
-    w_out_t[:, : w_out_ref.shape[1]] = w_out_ref[...]
-    turned(mix_ref, mix_t)
-    diagonal = lax.broadcasted_iota(jnp.int32, (channels, channels), 0) == lax.broadcasted_iota(
-        jnp.int32, (channels, channels), 1)
-    gain_col[...] = jnp.broadcast_to(
-        jnp.sum(jnp.where(diagonal, gain_ref[...], 0.0), axis=1, keepdims=True), (channels, LANES))
+        for u in range(0, step, 2):
+            rings = []
+            for c in (group * step + u, group * step + u + 1):
+                rim = jnp.broadcast_to(comb32[pl.ds(c, 1), :], (half, LANES))
+                for bit in (1, 2, 4):
+                    rim = jnp.where(lax.rem(index[:half] // bit, 2) == 1, pltpu.roll(rim, LANES - 8 * bit, 1), rim)
+                rim = jnp.concatenate([rim, pltpu.roll(rim, LANES - 8 * half, 1)], axis=0)
+                at = pl.multiple_of(c * rows, rows)
+                rings.append([flat[h, pl.ds(at, rows), :].astype(WORK) for h in range(tiles)] + [rim.astype(WORK)])
+            totals = product(group * step + u, 0, rings, lambda block: block.astype(BF16))
+            for n, total in enumerate(totals):
+                at = pl.multiple_of((group * step + u + n) * rows, rows)
+                for h in range(tiles):
+                    depth[h, pl.ds(at, rows), :] = total[:, h * LANES : (h + 1) * LANES]
 
     def edges_of(packed, i):
         return pltpu.roll(packed, LANES - 8 * i, 1) if i else packed
@@ -268,7 +288,7 @@
         halo[tiles, pl.ds(at, channels, stride=half), :] = rim
 
     def await_halo():
-        loads[3].wait()
+        loads[2].wait()
 
         @pl.when(lat > 0)
         def _():
@@ -312,14 +332,17 @@
 
         @pl.loop(0, channels // step)
         def _(group):
-            for u in range(step):
-                c = group * step + u
-                spot = pl.ds(pl.multiple_of(c * half, half), half)
-                ring = [jnp.concatenate([halo[h, spot, :]] * 2, axis=0).astype(WORK) for h in range(tiles + 1)]
-                total = product(c, 1, ring)
-                at = pl.multiple_of(c * rows, rows)
-                for h in range(tiles):
-                    depth[h, pl.ds(at, rows), :] += total[:, h * LANES : (h + 1) * LANES]
+            for u in range(0, step, 2):
+                rings = []
+                for c in (group * step + u, group * step + u + 1):
+                    spot = pl.ds(pl.multiple_of(c * half, half), half)
+                    rings.append([halo[h, spot, :] for h in range(tiles + 1)])
+                totals = product(
+                    group * step + u, 1, rings, lambda block: jnp.concatenate([block, block], axis=0).astype(BF16))
+                for n, total in enumerate(totals):
+                    at = pl.multiple_of((group * step + u + n) * rows, rows)
+                    for h in range(tiles):
+                        depth[h, pl.ds(at, rows), :] += total[:, h * LANES : (h + 1) * LANES]
 
     here = pl.ds(pl.multiple_of(lon * cols, LANES), cols)
 
@@ -339,9 +362,11 @@
             back.at[chunk, :, pl.ds(pl.multiple_of(q * cols, LANES), cols)], spatial.at[chunk * lon_n + lon],
             in_send.at[s], in_recv.at[s], device_id={"lon": q})
 
-    def mix_rows(chunk):
-        @pl.loop(0, lon_n // 2)
-        def _(pair):
+    def mix_rows(first, last):
+        @pl.loop(first * (lon_n // 2), last * (lon_n // 2))
+        def _(at):
+            chunk = at // (lon_n // 2)
+            pair = lax.rem(at, lon_n // 2)
             k = lon_n - 1 - 2 * pair
             one, two = row_at(chunk, target(k)), row_at(chunk, target(k - 1))
             x = jnp.concatenate(
@@ -385,39 +410,43 @@
         spatial[chunk * lon_n + lon] = back[chunk, :, here]
 
     def finish(chunk):
-        @pl.loop(0, lon_n)
-        def _(k):
-            @pl.when(k > 0)
+        @pl.loop(0, lon_n // 2)
+        def _(pair):
+            k = 2 * pair
+
+            @pl.when(pair > 0)
             def _():
                 send_back(chunk, k).wait_recv()
 
-            pos = source(k)
-            row = row_at(chunk, pos)
-            mixed = jnp.dot(mix_t[...], spatial[chunk * lon_n + pos], preferred_element_type=F32)
-            wet_row = mask_ref[pl.ds(row, 1), :].astype(F32)
-            val = wet_row * (res[row].astype(F32) + mixed)
-            for h in range(tiles):
-                flat_out[h, pl.ds(row, channels, stride=rows), :] = val[:, h * LANES : (h + 1) * LANES]
-
-    halo_done = False
-    for chunk in range(per):
-        out_rows = [(chunk * lon_n + q + HALO) % rows for q in range(lon_n)]
-        if not halo_done and (min(out_rows) < HALO or max(out_rows) >= rows - HALO):
-            await_halo()
-            halo_done = True
-        mix_rows(chunk)
-
-    loads[8].wait()
+            send_back(chunk, k + 1).wait_recv()
+            spots = [source(k), source(k + 1)]
+            points = jnp.concatenate([spatial[chunk * lon_n + pos] for pos in spots], axis=1)
+            mixed = jnp.dot(mix_t[...], points, preferred_element_type=F32)
+            for n, pos in enumerate(spots):
+                row = row_at(chunk, pos)
+                wet_row = mask_ref[pl.ds(row, 1), :].astype(F32)
+                val = wet_row * (res[row].astype(F32) + mixed[:, n * cols : (n + 1) * cols])
+                for h in range(tiles):
+                    flat_out[h, pl.ds(row, channels, stride=rows), :] = val[:, h * LANES : (h + 1) * LANES]
+
+    needs = [
+        any((chunk * lon_n + q + HALO) % rows < HALO or (chunk * lon_n + q + HALO) % rows >= rows - HALO for q in range(lon_n))
+        for chunk in range(per)]
+    early = needs.index(True)
+    if early:
+        mix_rows(0, early)
+    loads[7].wait()
     wide = modes // LANES
     for p in range(2):
         for t in range(wide):
             spec_ref[p, :, t * LANES : (t + 1) * LANES] = spec_raw[pl.ds(2 * t + p, channels, stride=2 * wide), :]
-    loads[9].wait()
-
-    for chunk in range(per):
-        spectral(chunk)
-    for chunk in range(per):
-        finish(chunk)
+    loads[8].wait()
+    if early:
+        pl.loop(0, early)(spectral)
+    await_halo()
+    mix_rows(early, per)
+    pl.loop(early, per)(spectral)
+    pl.loop(0, per)(finish)
 
     @pl.loop(0, channels // step)
     def _(group):
@@ -452,7 +481,7 @@
     peers = lon_n - 1
     return pl.pallas_call(
         functools.partial(kernel, sizes),
-        out_shape=jax.ShapeDtypeStruct(field.shape, BF16),
+        out_shape=pltpu.VMEM(field.shape, BF16),
         in_specs=[pl.BlockSpec(memory_space=pltpu.HBM)] * len(operands),
         out_specs=pl.BlockSpec(memory_space=pltpu.VMEM),
         scratch_shapes=[
@@ -477,7 +506,7 @@
             pltpu.VMEM((channels, hid_up), BF16),
             pltpu.VMEM((channels, channels), BF16),
             pltpu.VMEM((channels, LANES), F32),
-            dma((len(operands),)),
+            dma((2 * len(operands) + channels,)),
             *[dma((2,))] * 6,
             *[dma((peers,))] * 2,
             *[dma((peers * per,))] * 4,

time: 54.3 us -> 45.1 us (0.83)
  the two profiles are of different devices: /device:TPU:28 before, /device:TPU:0 now
where the time goes in v2:
time: 45.1 us; the launch traced here: 44.4 us
  Pallas kernels  43.3 us (96%)
  local copies, waits for them, and re-layouts  1.03 us (2%)
    pallas_call x1, Pallas kernels, local(): pl.pallas_call(functools.partial(kernel, sizes), out_shape=pltpu.VMEM(fie...  43.3 us
    unnamed x1, local copies, waits for them, and re-layouts  1.03 us

profile of v2, /device:TPU:0, one launch (start us, length us, event | category | flops | bytes accessed | tf_op | source)
XLA Modules:
  0.0 44.4 jit_solution(8245878620366979746)
XLA Ops:
  0.0 43.3 %block.1 = bf16[150,16,256]{2,1,0:T(8,128)(2,1)S(1)} custom-call(bf16[150,16,256]{2,1,0:T(8,128)(2,1)} %field_hbm.1, s32[16,256]{1,0:T(8,128)} %mask_hbm.1, s32[1,1024]{1,0:T(1,128)} %bitcast.14, f32[7,7,150]{2,1,0:T(8,128)} %bitcast.13, f32[1,150]{1,0:T(1,128)} %bitcast.15, bf16[150,600]{1,0:T(8,128)(2,1)} %w_in_hbm.1, bf16[150,600]{1,0:T(8,128)(2,1)} %bitcast.12, ...), custom_call_target="tpu_custom_call" | custom-call | tf_op jit(solution)/shard_map/block/pallas_call | solution.py:482
  43.3 1.0 %copy.13 = bf16[150,16,256]{2,1,0:T(8,128)(2,1)} copy(bf16[150,16,256]{2,1,0:T(8,128)(2,1)S(1)} %block.1) | data formatting | bytes 2457600

commit v3 on v2

--- a/solution.py
+++ b/solution.py
@@ -15,6 +15,8 @@
 HALO = 3
 LANES = 128
 WORK = BF16
+GELU_LINE = math.sqrt(2.0 / math.pi)
+GELU_CUBE = 0.044715 * GELU_LINE
 STEP = 30
 VMEM_LIMIT = 58 * 1024 * 1024
 
@@ -87,10 +89,8 @@
     def _():
         pl.semaphore_signal(barrier, inc=1, device_id={"lat": lat + 1})
 
-    for load in loads[2:]:
-        load.start()
-
     lane = lax.broadcasted_iota(jnp.int32, (rows, LANES), 1)
+    half = rows // 2
     loads[1].wait()
     wet = mask_ref[...].astype(F32)
 
@@ -106,8 +106,13 @@
             for h in range(tiles):
                 flat[h, pl.ds(at, rows), :] = parts[h]
             edge = jnp.where(lane < HALO, parts[0], jnp.where(lane >= LANES - HALO, parts[-1], 0.0))
-            edge = pltpu.roll(edge, 0, 1, stride=8, stride_axis=0)
-            edge32[pl.ds(c, 1), :] = jnp.sum(edge, axis=0, keepdims=True)
+            edge = edge[:half] + pltpu.roll(edge[half:], LANES - 8 * half, 1)
+            for hop in (4, 2, 1):
+                edge = edge + pltpu.roll(pltpu.roll(edge, half - hop, 0), LANES - 8 * hop, 1)
+            edge32[pl.ds(c, 1), :] = edge[:1]
+
+    for load in loads[2:]:
+        load.start()
 
     edge_mine[...] = edge32[...].astype(BF16)
 
@@ -178,7 +183,6 @@
     slot = lax.rem(lane, rows)
     index = lax.broadcasted_iota(jnp.int32, (rows, LANES), 0)
     band = jnp.abs(slot - index) <= HALO
-    half = rows // 2
     low_slot = slot[:half] < HALO
     high_slot = (slot[:half] >= half + HALO) & (slot[:half] < half + 2 * HALO)
 
@@ -267,10 +271,8 @@
         for u in range(0, step, 2):
             rings = []
             for c in (group * step + u, group * step + u + 1):
-                rim = jnp.broadcast_to(comb32[pl.ds(c, 1), :], (half, LANES))
-                for bit in (1, 2, 4):
-                    rim = jnp.where(lax.rem(index[:half] // bit, 2) == 1, pltpu.roll(rim, LANES - 8 * bit, 1), rim)
-                rim = jnp.concatenate([rim, pltpu.roll(rim, LANES - 8 * half, 1)], axis=0)
+                rim = jnp.broadcast_to(comb32[pl.ds(c, 1), :], (rows, LANES))
+                rim = pltpu.roll(rim, 0, 1, stride=8, stride_axis=0)
                 at = pl.multiple_of(c * rows, rows)
                 rings.append([flat[h, pl.ds(at, rows), :].astype(WORK) for h in range(tiles)] + [rim.astype(WORK)])
             totals = product(group * step + u, 0, rings, lambda block: block.astype(BF16))
@@ -280,7 +282,7 @@
                     depth[h, pl.ds(at, rows), :] = total[:, h * LANES : (h + 1) * LANES]
 
     def edges_of(packed, i):
-        return pltpu.roll(packed, LANES - 8 * i, 1) if i else packed
+        return pltpu.roll(packed, 8 * i, 1) if i else packed
 
     def put_halo(at, value, rim):
         for h in range(tiles):
@@ -330,6 +332,7 @@
                 row = jnp.dot(top_all[HALO - 1 - r], pick, preferred_element_type=F32)
                 put_halo(HALO + r, row[:, :cols], row[:, cols:])
 
+    def halo_conv():
         @pl.loop(0, channels // step)
         def _(group):
             for u in range(0, step, 2):
@@ -377,11 +380,12 @@
             gain = jnp.concatenate([gain_col[...]] * (2 * tiles), axis=1)
             normed = (centred * lax.rsqrt(var + 1e-06) * gain).astype(BF16)
             pre = jnp.dot(w_in_t[...], normed, preferred_element_type=F32)
-            hidden = jax.nn.gelu(pre, approximate=True).astype(BF16)
+            inner = pre * (GELU_CUBE * (pre * pre) + GELU_LINE)
+            hidden = (pre + pre * jnp.tanh(inner)).astype(BF16)
             branch = jnp.dot(w_out_t[...], hidden, preferred_element_type=F32)
             for n, row in enumerate((one, two)):
                 wet_row = mask_ref[pl.ds(row, 1), :].astype(F32)
-                part = branch[:, n * cols : (n + 1) * cols]
+                part = 0.5 * branch[:, n * cols : (n + 1) * cols]
                 res[row] = (wet_row * (own[row].astype(F32) + part)).astype(BF16)
             send_row(chunk, k).start()
 
@@ -441,12 +445,25 @@
         for t in range(wide):
             spec_ref[p, :, t * LANES : (t + 1) * LANES] = spec_raw[pl.ds(2 * t + p, channels, stride=2 * wide), :]
     loads[8].wait()
+    if early > 1:
+        pl.loop(0, early - 1)(spectral)
+    await_halo()
     if early:
-        pl.loop(0, early)(spectral)
-    await_halo()
+        spectral(early - 1)
+    halo_conv()
     mix_rows(early, per)
     pl.loop(early, per)(spectral)
-    pl.loop(0, per)(finish)
+    if per > 1:
+        pl.loop(0, per - 1)(finish)
+
+    @pl.loop(0, per * (lon_n - 1))
+    def _(at):
+        chunk = at // (lon_n - 1)
+        k = lon_n - 1 - lax.rem(at, lon_n - 1)
+        send_row(chunk, k).wait_send()
+        send_back(chunk, k).wait_send()
+
+    finish(per - 1)
 
     @pl.loop(0, channels // step)
     def _(group):
@@ -455,11 +472,6 @@
             at = pl.multiple_of(c * rows, rows)
             for h in range(tiles):
                 out_ref[c, :, h * LANES : (h + 1) * LANES] = flat_out[h, pl.ds(at, rows), :].astype(BF16)
-
-    for chunk in range(per):
-        for k in range(lon_n - 1, 0, -1):
-            send_row(chunk, k).wait_send()
-            send_back(chunk, k).wait_send()
 
 
 def local(lat_n, lon_n, field, land_mask, fold_partner, dw_kernel, norm_gain, w_in, w_out, spec_gain, mix_weight):

time: 45.1 us -> 44.3 us (0.982); the launches traced: 44.4 us -> 44.1 us
  no operation moved by 1% of the time
where the time goes in v3:
time: 44.3 us; the launch traced here: 44.1 us
  Pallas kernels  43.1 us (97%)
  local copies, waits for them, and re-layouts  1.03 us (2%)
    pallas_call x1, Pallas kernels, local(): pl.pallas_call(functools.partial(kernel, sizes), out_shape=pltpu.VMEM(fie...  43.1 us
    unnamed x1, local copies, waits for them, and re-layouts  1.03 us

profile of v3, /device:TPU:0, one launch (start us, length us, event | category | flops | bytes accessed | tf_op | source)
XLA Modules:
  0.0 44.1 jit_solution(16383169888168040405)
XLA Ops:
  0.0 43.1 %block.1 = bf16[150,16,256]{2,1,0:T(8,128)(2,1)S(1)} custom-call(bf16[150,16,256]{2,1,0:T(8,128)(2,1)} %field_hbm.1, s32[16,256]{1,0:T(8,128)} %mask_hbm.1, s32[1,1024]{1,0:T(1,128)} %bitcast.14, f32[7,7,150]{2,1,0:T(8,128)} %bitcast.13, f32[1,150]{1,0:T(1,128)} %bitcast.15, bf16[150,600]{1,0:T(8,128)(2,1)} %w_in_hbm.1, bf16[150,600]{1,0:T(8,128)(2,1)} %bitcast.12, ...), custom_call_target="tpu_custom_call" | custom-call | tf_op jit(solution)/shard_map/block/pallas_call | solution.py:494
  43.1 1.0 %copy.13 = bf16[150,16,256]{2,1,0:T(8,128)(2,1)} copy(bf16[150,16,256]{2,1,0:T(8,128)(2,1)S(1)} %block.1) | data formatting | bytes 2457600

commit v4 on v3

--- a/solution.py
+++ b/solution.py
@@ -28,6 +28,10 @@
     angles = angles.astype(np.float64)
     table = np.concatenate([np.cos(angles), -np.sin(angles)], axis=1).astype(np.float32)
     return (table * factor).astype(BF16)
+
+
+def loop_step(channels):
+    return max(u for u in range(2, STEP + 1, 2) if channels % u == 0)
 
 
 def kernel(
@@ -46,7 +50,7 @@
     lon_points = cols * lon_n
     tiles = cols // LANES
     per = rows // lon_n
-    step = max(u for u in range(2, STEP + 1, 2) if channels % u == 0)
+    step = loop_step(channels)
     lat = lax.axis_index("lat")
     lon = lax.axis_index("lon")
     left = lax.rem(lon + lon_n - 1, lon_n)
@@ -365,37 +369,49 @@
             back.at[chunk, :, pl.ds(pl.multiple_of(q * cols, LANES), cols)], spatial.at[chunk * lon_n + lon],
             in_send.at[s], in_recv.at[s], device_id={"lon": q})
 
+    def mix_some(chunk, ks):
+        places = [row_at(chunk, target(k)) for k in ks]
+        x = jnp.concatenate(
+            [depth[h, pl.ds(row, channels, stride=rows), :] for row in places for h in range(tiles)], axis=1)
+        mean = jnp.sum(x, axis=0, keepdims=True) * (1.0 / channels)
+        centred = x - mean
+        var = jnp.sum(centred * centred, axis=0, keepdims=True) * (1.0 / channels)
+        gain = jnp.concatenate([gain_col[...]] * (len(ks) * tiles), axis=1)
+        normed = (centred * lax.rsqrt(var + 1e-06) * gain).astype(BF16)
+        pre = jnp.dot(w_in_t[...], normed, preferred_element_type=F32)
+        inner = pre * (GELU_CUBE * (pre * pre) + GELU_LINE)
+        hidden = (pre + pre * jnp.tanh(inner)).astype(BF16)
+        branch = jnp.dot(w_out_t[...], hidden, preferred_element_type=F32)
+        for n, row in enumerate(places):
+            wet_row = mask_ref[pl.ds(row, 1), :].astype(F32)
+            part = 0.5 * branch[:, n * cols : (n + 1) * cols]
+            res[row] = (wet_row * (own[row].astype(F32) + part)).astype(BF16)
+        return places
+
+    half_ring = lon_n // 2
+
     def mix_rows(first, last):
-        @pl.loop(first * (lon_n // 2), last * (lon_n // 2))
+        @pl.loop(first, last)
         def _(at):
-            chunk = at // (lon_n // 2)
-            pair = lax.rem(at, lon_n // 2)
+            chunk = at // half_ring
+            pair = lax.rem(at, half_ring)
             k = lon_n - 1 - 2 * pair
-            one, two = row_at(chunk, target(k)), row_at(chunk, target(k - 1))
-            x = jnp.concatenate(
-                [depth[h, pl.ds(row, channels, stride=rows), :] for row in (one, two) for h in range(tiles)], axis=1)
-            mean = jnp.sum(x, axis=0, keepdims=True) * (1.0 / channels)
-            centred = x - mean
-            var = jnp.sum(centred * centred, axis=0, keepdims=True) * (1.0 / channels)
-            gain = jnp.concatenate([gain_col[...]] * (2 * tiles), axis=1)
-            normed = (centred * lax.rsqrt(var + 1e-06) * gain).astype(BF16)
-            pre = jnp.dot(w_in_t[...], normed, preferred_element_type=F32)
-            inner = pre * (GELU_CUBE * (pre * pre) + GELU_LINE)
-            hidden = (pre + pre * jnp.tanh(inner)).astype(BF16)
-            branch = jnp.dot(w_out_t[...], hidden, preferred_element_type=F32)
-            for n, row in enumerate((one, two)):
-                wet_row = mask_ref[pl.ds(row, 1), :].astype(F32)
-                part = 0.5 * branch[:, n * cols : (n + 1) * cols]
-                res[row] = (wet_row * (own[row].astype(F32) + part)).astype(BF16)
+            _, two = mix_some(chunk, (k, k - 1))
             send_row(chunk, k).start()
 
-            @pl.when(pair < lon_n // 2 - 1)
+            @pl.when(pair < half_ring - 1)
             def _():
                 send_row(chunk, k - 1).start()
 
-            @pl.when(pair == lon_n // 2 - 1)
+            @pl.when(pair == half_ring - 1)
             def _():
                 by_rows[chunk, :, here] = res[two]
+
+    def mix_first():
+        @pl.loop(0, 2)
+        def _(at):
+            mix_some(0, (lon_n - 1 - at,))
+            send_row(0, lon_n - 1 - at).start()
 
     def spectral(chunk):
         for k in range(lon_n - 1, 0, -1):
@@ -438,7 +454,10 @@
         for chunk in range(per)]
     early = needs.index(True)
     if early:
-        mix_rows(0, early)
+        alone = int(half_ring > 1)
+        if alone:
+            mix_first()
+        mix_rows(alone, early * half_ring)
     loads[7].wait()
     wide = modes // LANES
     for p in range(2):
@@ -451,7 +470,7 @@
     if early:
         spectral(early - 1)
     halo_conv()
-    mix_rows(early, per)
+    mix_rows(early * half_ring, per * half_ring)
     pl.loop(early, per)(spectral)
     if per > 1:
         pl.loop(0, per - 1)(finish)
@@ -487,6 +506,7 @@
     wide = modes // LANES
     spec = spec_gain.transpose(1, 0, 2).reshape(channels, 2, wide, LANES).transpose(0, 2, 1, 3).reshape(-1, LANES)
     per = rows // lon_n
+    groups = channels // loop_step(channels)
     sizes = (channels, rows, cols, lat_n, lon_n, modes)
     operands = (field, land_mask, fold_partner[None, :], taps, norm_gain[None, :], w_in, w_out.T, mix_weight, spec, table)
     dma = pltpu.SemaphoreType.DMA
@@ -518,7 +538,7 @@
             pltpu.VMEM((channels, hid_up), BF16),
             pltpu.VMEM((channels, channels), BF16),
             pltpu.VMEM((channels, LANES), F32),
-            dma((2 * len(operands) + channels,)),
+            dma((len(operands) + groups,)),
             *[dma((2,))] * 6,
             *[dma((peers,))] * 2,
             *[dma((peers * per,))] * 4,

time: 44.3 us -> 42.6 us (0.962)
  Pallas kernels: 43.1 us -> 41.5 us
    pallas_call x1, Pallas kernels: 43.1 us -> 41.5 us  [local(): pl.pallas_call(functools.partial(kernel, sizes), out_shape=pltpu.VMEM(fie...]
where the time goes in v4:
time: 42.6 us; the launch traced here: 42.5 us
  Pallas kernels  41.5 us (97%)
  local copies, waits for them, and re-layouts  1.03 us (2%)
    pallas_call x1, Pallas kernels, local(): pl.pallas_call(functools.partial(kernel, sizes), out_shape=pltpu.VMEM(fie...  41.5 us
    unnamed x1, local copies, waits for them, and re-layouts  1.03 us

profile of v4, /device:TPU:0, one launch (start us, length us, event | category | flops | bytes accessed | tf_op | source)
XLA Modules:
  0.0 42.5 jit_solution(16721545858044575060)
XLA Ops:
  0.0 41.5 %block.1 = bf16[150,16,256]{2,1,0:T(8,128)(2,1)S(1)} custom-call(bf16[150,16,256]{2,1,0:T(8,128)(2,1)} %field_hbm.1, s32[16,256]{1,0:T(8,128)} %mask_hbm.1, s32[1,1024]{1,0:T(1,128)} %bitcast.14, f32[7,7,150]{2,1,0:T(8,128)} %bitcast.13, f32[1,150]{1,0:T(1,128)} %bitcast.15, bf16[150,600]{1,0:T(8,128)(2,1)} %w_in_hbm.1, bf16[150,600]{1,0:T(8,128)(2,1)} %bitcast.12, ...), custom_call_target="tpu_custom_call" | custom-call | tf_op jit(solution)/shard_map/block/pallas_call | solution.py:514
  41.5 1.0 %copy.13 = bf16[150,16,256]{2,1,0:T(8,128)(2,1)} copy(bf16[150,16,256]{2,1,0:T(8,128)(2,1)S(1)} %block.1) | data formatting | bytes 2457600

commit v5 on v4

--- a/solution.py
+++ b/solution.py
@@ -98,8 +98,7 @@
     loads[1].wait()
     wet = mask_ref[...].astype(F32)
 
-    @pl.loop(0, channels // step)
-    def _(group):
+    def mask_group(group):
         for u in range(step):
             c = group * step + u
             if u == 0:
@@ -115,20 +114,30 @@
                 edge = edge + pltpu.roll(pltpu.roll(edge, half - hop, 0), LANES - 8 * hop, 1)
             edge32[pl.ds(c, 1), :] = edge[:1]
 
+    first_groups = -(-groups // 2)
+    split_at = first_groups * step // 16 * 16
+    parts = (slice(0, split_at), slice(split_at, channels))
+
+    def edge_copy(n, way):
+        some = pl.ds(parts[n].start, parts[n].stop - parts[n].start)
+        put = (edge_right, edge_left)[way]
+        return pltpu.make_async_remote_copy(
+            edge_mine.at[some], put.at[some], edge_send.at[2 * n + way], edge_recv.at[2 * n + way],
+            device_id={"lon": (left, right)[way]})
+
+    def send_edges(n):
+        edge_mine[parts[n], :] = edge32[parts[n], :].astype(BF16)
+        edge_copy(n, 0).start()
+        edge_copy(n, 1).start()
+
+    count = lon_n - 1 + jnp.where(lat > 0, 1, 0) + jnp.where(lat < lat_n - 1, 1, 0)
+    pl.loop(0, first_groups)(mask_group)
+    pl.semaphore_wait(barrier, count)
+    send_edges(0)
+    pl.loop(first_groups, groups)(mask_group)
+    send_edges(1)
     for load in loads[2:]:
         load.start()
-
-    edge_mine[...] = edge32[...].astype(BF16)
-
-    count = lon_n - 1 + jnp.where(lat > 0, 1, 0) + jnp.where(lat < lat_n - 1, 1, 0)
-    pl.semaphore_wait(barrier, count)
-
-    to_left = pltpu.make_async_remote_copy(
-        edge_mine, edge_right, edge_send.at[0], edge_recv.at[0], device_id={"lon": left})
-    to_right = pltpu.make_async_remote_copy(
-        edge_mine, edge_left, edge_send.at[1], edge_recv.at[1], device_id={"lon": right})
-    to_left.start()
-    to_right.start()
 
     def own_row(i):
         for h in range(tiles):
@@ -227,20 +236,14 @@
     for i in range(HALO, rows - HALO):
         own_row(i)
 
-    to_left.wait()
-    to_right.wait()
-    near = lax.rem(lax.broadcasted_iota(jnp.int32, (channels, LANES), 1), 8) < 4
-    both = jnp.where(near, edge_right[...].astype(F32), edge_left[...].astype(F32))
-    comb[...] = both.astype(BF16)
-    comb32[...] = both
-
-    @pl.when(lat > 0)
-    def _():
-        comb_down.start()
-
-    @pl.when(lat < lat_n - 1)
-    def _():
-        comb_up.start()
+    def take_edges(n):
+        edge_copy(n, 0).wait()
+        edge_copy(n, 1).wait()
+        part = parts[n]
+        near = lax.rem(lax.broadcasted_iota(jnp.int32, (part.stop - part.start, LANES), 1), 8) < 4
+        both = jnp.where(near, edge_right[part, :].astype(F32), edge_left[part, :].astype(F32))
+        comb[part, :] = both.astype(BF16)
+        comb32[part, :] = both
 
     def shifted(ring, finish_block):
         high = ring[0].shape[0]
@@ -270,8 +273,7 @@
         total = jnp.dot(weights, points, preferred_element_type=F32)
         return total[:rows] + total[rows : 2 * rows], total[2 * rows : 3 * rows] + total[3 * rows :]
 
-    @pl.loop(0, channels // step)
-    def _(group):
+    def conv_group(group):
         for u in range(0, step, 2):
             rings = []
             for c in (group * step + u, group * step + u + 1):
@@ -284,6 +286,20 @@
                 at = pl.multiple_of((group * step + u + n) * rows, rows)
                 for h in range(tiles):
                     depth[h, pl.ds(at, rows), :] = total[:, h * LANES : (h + 1) * LANES]
+
+    take_edges(0)
+    pl.loop(0, split_at // step)(conv_group)
+    take_edges(1)
+
+    @pl.when(lat > 0)
+    def _():
+        comb_down.start()
+
+    @pl.when(lat < lat_n - 1)
+    def _():
+        comb_up.start()
+
+    pl.loop(split_at // step, groups)(conv_group)
 
     def edges_of(packed, i):
         return pltpu.roll(packed, 8 * i, 1) if i else packed
@@ -407,11 +423,13 @@
             def _():
                 by_rows[chunk, :, here] = res[two]
 
-    def mix_first():
-        @pl.loop(0, 2)
+    alone = int(half_ring > 1)
+
+    def mix_first(chunk):
+        @pl.loop(0, 2 * alone)
         def _(at):
-            mix_some(0, (lon_n - 1 - at,))
-            send_row(0, lon_n - 1 - at).start()
+            mix_some(chunk, (lon_n - 1 - at,))
+            send_row(chunk, lon_n - 1 - at).start()
 
     def spectral(chunk):
         for k in range(lon_n - 1, 0, -1):
@@ -454,9 +472,7 @@
         for chunk in range(per)]
     early = needs.index(True)
     if early:
-        alone = int(half_ring > 1)
-        if alone:
-            mix_first()
+        mix_first(0)
         mix_rows(alone, early * half_ring)
     loads[7].wait()
     wide = modes // LANES
@@ -470,7 +486,8 @@
     if early:
         spectral(early - 1)
     halo_conv()
-    mix_rows(early * half_ring, per * half_ring)
+    mix_first(early)
+    mix_rows(early * half_ring + alone, per * half_ring)
     pl.loop(early, per)(spectral)
     if per > 1:
         pl.loop(0, per - 1)(finish)
@@ -539,7 +556,8 @@
             pltpu.VMEM((channels, channels), BF16),
             pltpu.VMEM((channels, LANES), F32),
             dma((len(operands) + groups,)),
-            *[dma((2,))] * 6,
+            *[dma((4,))] * 2,
+            *[dma((2,))] * 4,
             *[dma((peers,))] * 2,
             *[dma((peers * per,))] * 4,
         ],

time: 42.6 us -> 42.2 us (level)
  Pallas kernels: 41.5 us -> 41 us
    pallas_call x1, Pallas kernels: 41.5 us -> 41 us  [local(): pl.pallas_call(functools.partial(kernel, sizes), out_shape=pltpu.VMEM(fie...]
where the time goes in v5:
time: 42.2 us; the launch traced here: 42.1 us
  Pallas kernels  41 us (97%)
  local copies, waits for them, and re-layouts  1.03 us (2%)
    pallas_call x1, Pallas kernels, local(): pl.pallas_call(functools.partial(kernel, sizes), out_shape=pltpu.VMEM(fie...  41 us
    unnamed x1, local copies, waits for them, and re-layouts  1.03 us

profile of v5, /device:TPU:0, one launch (start us, length us, event | category | flops | bytes accessed | tf_op | source)
XLA Modules:
  0.0 42.1 jit_solution(15723319312070875723)
XLA Ops:
  0.0 41.0 %block.1 = bf16[150,16,256]{2,1,0:T(8,128)(2,1)S(1)} custom-call(bf16[150,16,256]{2,1,0:T(8,128)(2,1)} %field_hbm.1, s32[16,256]{1,0:T(8,128)} %mask_hbm.1, s32[1,1024]{1,0:T(1,128)} %bitcast.14, f32[7,7,150]{2,1,0:T(8,128)} %bitcast.13, f32[1,150]{1,0:T(1,128)} %bitcast.15, bf16[150,600]{1,0:T(8,128)(2,1)} %w_in_hbm.1, bf16[150,600]{1,0:T(8,128)(2,1)} %bitcast.12, ...), custom_call_target="tpu_custom_call" | custom-call | tf_op jit(solution)/shard_map/block/pallas_call | solution.py:531
  41.0 1.0 %copy.13 = bf16[150,16,256]{2,1,0:T(8,128)(2,1)} copy(bf16[150,16,256]{2,1,0:T(8,128)(2,1)S(1)} %block.1) | data formatting | bytes 2457600

commit v6 on v5

--- a/solution.py
+++ b/solution.py
@@ -68,7 +68,7 @@
 
     whole = (
         (taps_hbm, taps_ref), (mask_hbm, mask_ref), (fold_hbm, fold_ref), (gain_hbm, gain_ref), (w_in_hbm, w_in_ref),
-        (w_out_hbm, w_out_ref), (mix_hbm, mix_ref), (spec_hbm, spec_raw), (table_hbm, table_ref))
+        (w_out_hbm, w_out_ref), (mix_hbm, mix_ref), (spec_hbm, spec_raw.at[pl.ds(0, spec_hbm.shape[0])]), (table_hbm, table_ref))
     loads = [pltpu.make_async_copy(a, b, local_sem.at[n]) for n, (a, b) in enumerate(whole)]
     groups = channels // step
 
@@ -522,6 +522,7 @@
     taps = dw_kernel.transpose(1, 2, 0)
     wide = modes // LANES
     spec = spec_gain.transpose(1, 0, 2).reshape(channels, 2, wide, LANES).transpose(0, 2, 1, 3).reshape(-1, LANES)
+    room = -(-channels // 16) * 16
     per = rows // lon_n
     groups = channels // loop_step(channels)
     sizes = (channels, rows, cols, lat_n, lon_n, modes)
@@ -534,12 +535,14 @@
         in_specs=[pl.BlockSpec(memory_space=pltpu.HBM)] * len(operands),
         out_specs=pl.BlockSpec(memory_space=pltpu.VMEM),
         scratch_shapes=[
-            *[pltpu.VMEM(x.shape, x.dtype) for x in operands],
-            pltpu.VMEM((tiles, channels * rows, LANES), F32),
+            *[pltpu.VMEM(x.shape, x.dtype) for x in operands[:-2]],
+            pltpu.VMEM((room * 2 * wide, LANES), F32),
+            pltpu.VMEM(table.shape, BF16),
+            pltpu.VMEM((tiles, room * rows, LANES), F32),
             pltpu.VMEM((rows, channels, cols), BF16),
-            pltpu.VMEM((tiles, channels * rows, LANES), F32),
-            pltpu.VMEM((tiles, channels * rows, LANES), F32),
-            pltpu.VMEM((tiles + 1, channels * rows // 2, LANES), F32),
+            pltpu.VMEM((tiles, room * rows, LANES), F32),
+            pltpu.VMEM((tiles, room * rows, LANES), F32),
+            pltpu.VMEM((tiles + 1, room * rows // 2, LANES), F32),
             pltpu.VMEM((channels, 4 * rows, LANES), BF16),
             pltpu.VMEM((LANES, chan_up), F32),
             *[pltpu.VMEM((channels, LANES), F32)] * 4,

time: 42.2 us -> 42.2 us (level)
  no operation moved by 1% of the time
where the time goes in v6:
time: 42.2 us; the launch traced here: 42.1 us
  Pallas kernels  41 us (97%)
  local copies, waits for them, and re-layouts  1.03 us (2%)
    pallas_call x1, Pallas kernels, local(): pl.pallas_call(functools.partial(kernel, sizes), out_shape=pltpu.VMEM(fie...  41 us
    unnamed x1, local copies, waits for them, and re-layouts  1.03 us

profile of v6, /device:TPU:0, one launch (start us, length us, event | category | flops | bytes accessed | tf_op | source)
XLA Modules:
  0.0 42.1 jit_solution(3552614436885718064)
XLA Ops:
  0.0 41.0 %block.1 = bf16[150,16,256]{2,1,0:T(8,128)(2,1)S(1)} custom-call(bf16[150,16,256]{2,1,0:T(8,128)(2,1)} %field_hbm.1, s32[16,256]{1,0:T(8,128)} %mask_hbm.1, s32[1,1024]{1,0:T(1,128)} %bitcast.14, f32[7,7,150]{2,1,0:T(8,128)} %bitcast.13, f32[1,150]{1,0:T(1,128)} %bitcast.15, bf16[150,600]{1,0:T(8,128)(2,1)} %w_in_hbm.1, bf16[150,600]{1,0:T(8,128)(2,1)} %bitcast.12, ...), custom_call_target="tpu_custom_call" | custom-call | tf_op jit(solution)/shard_map/block/pallas_call | solution.py:532
  41.0 1.0 %copy.13 = bf16[150,16,256]{2,1,0:T(8,128)(2,1)} copy(bf16[150,16,256]{2,1,0:T(8,128)(2,1)S(1)} %block.1) | data formatting | bytes 2457600
